TPU v7x, 32 devices: a whole 2x2x4 slice. The times are simulated.
32 devices in a mesh: grid: 2 (over x), prow: 4 (over y, core), pcol: 4 (over z).
Axes of the slice: x: 2, y: 2, z: 4, core: 2. Of those that a mesh axis runs over, the one named last changes fastest.
Arguments:
- sub_rhs: float32 [2, 3, 64, 3072], P('grid', None, None, 'prow'), may hold values from -6 to 6
- root_rhs: float32 [64, 3072], P(None, 'prow'), may hold values from -6 to 6
- diag_inverse: bfloat16 [3, 3072, 6144], P(None, 'prow', ('grid', 'pcol'))
- root_inverse: bfloat16 [3072, 3072], P('prow', 'grid')
- inner_factor: bfloat16 [3, 6144, 3072], P(None, ('grid', 'pcol'), 'prow'), may hold values from -0.078125 to 0.078125
- inner_mask: int32 [3, 48, 24], P(None, ('grid', 'pcol')), may hold values 0 or 1
- root_factor: bfloat16 [3, 6144, 3072], P(None, ('grid', 'pcol'), 'prow'), may hold values from -0.078125 to 0.078125
- root_mask: int32 [3, 48, 24], P(None, ('grid', 'pcol')), may hold values 0 or 1
Outputs:
- sub_solution: float32 [3, 64, 6144], P(None, None, ('grid', 'pcol'))
- root_solution: float32 [64, 3072], P(None, 'grid')
Inputs may be any that keep to these rules, and one draw needn't show every extreme that they name: `inner_mask`: 1 keeps a tile of 128 x 128 entries, 0 makes it zero. `root_mask`: 1 keeps a tile of 128 x 128 entries, 0 makes it zero.
All inputs are finite; a program needn't handle non-finite values. No bound on the sum of `inner_mask` or of `root_mask` on one device may be relied on, other than what follows from the above.
Results may differ from a plain program's by a relative error of at most 0.0065.
Values sent between devices are 32-bit elements; how exact they have to be, the bound alone decides.
A program may use at most 64 MiB of HBM per device.

v0:
```python
import jax
import jax.numpy as jnp
from jax import lax
from jax.sharding import PartitionSpec as P

NS = 3072
LEVELS = 3
TILE = 128


def from_partner(shard, axis, bit):
    return lax.ppermute(shard, axis, [(i, i ^ 1 << bit) for i in range(lax.axis_size(axis))])


def selector(positions, count):
    return (positions[:, None] // TILE == jnp.arange(count)[None, :]).astype(jnp.float32)


def masked(factor, mask, row_select, col_select):
    expanded = jnp.dot(jnp.dot(row_select, mask.astype(jnp.float32)), col_select.T)
    return factor * expanded.astype(jnp.bfloat16)


def solve_block(residual, inverse):
    partial_sum = jnp.dot(
        residual.astype(jnp.bfloat16), inverse, preferred_element_type=jnp.float32
    )
    return lax.psum(partial_sum, "prow")


def group_sum(partial_sum, owners):
    summed = partial_sum
    for bit_number in range(owners.bit_length() - 1):
        summed = summed + from_partner(summed, "pcol", bit_number)
    return summed


def shards(
    sub_rhs, root_rhs, diag_inverse, root_inverse, inner_factor, inner_mask, root_factor, root_mask
):
    rows_here = inner_factor.shape[1]
    out_cols = inner_factor.shape[2]
    owners = NS // rows_here
    own_tree = lax.axis_index("pcol") // owners
    col_positions = lax.axis_index("prow") * out_cols + jnp.arange(out_cols)
    row_select = selector(jnp.arange(rows_here), inner_mask.shape[1])
    col_select = selector(col_positions, inner_mask.shape[2])
    own_rhs = lax.dynamic_index_in_dim(sub_rhs, own_tree, 0, keepdims=False)
    kept = []
    solved_all = []
    pair = 0
    for level in range(LEVELS):
        residual = own_rhs[level]
        if level > 0:
            local_update = jnp.zeros(residual.shape, jnp.float32)
            for source in range(level):
                factor_tile = masked(inner_factor[pair], inner_mask[pair], row_select, col_select)
                local_update = local_update + jnp.dot(
                    kept[source], factor_tile, preferred_element_type=jnp.float32
                )
                pair += 1
            residual = residual - group_sum(local_update, owners)
        solved = solve_block(residual, diag_inverse[level])
        solved_all.append(solved)
        kept.append(solved.astype(jnp.bfloat16))
    root_local = jnp.zeros(root_rhs.shape, jnp.float32)
    for source in range(LEVELS):
        factor_tile = masked(root_factor[source], root_mask[source], row_select, col_select)
        root_local = root_local + jnp.dot(
            kept[source], factor_tile, preferred_element_type=jnp.float32
        )
    across = lax.psum(root_local, "pcol")
    root_update = lax.psum(across, "grid")
    root_solution = solve_block(root_rhs - root_update, root_inverse)
    return (jnp.stack(solved_all), root_solution)


def solution(mesh):
    return jax.shard_map(
        shards,
        mesh=mesh,
        in_specs=(
            P("grid", None, None, "prow"),
            P(None, "prow"),
            P(None, "prow", ("grid", "pcol")),
            P("prow", "grid"),
            P(None, ("grid", "pcol"), "prow"),
            P(None, ("grid", "pcol"), None),
            P(None, ("grid", "pcol"), "prow"),
            P(None, ("grid", "pcol"), None),
        ),
        out_specs=(P(None, None, ("grid", "pcol")), P(None, "grid")),
        check_vma=False,
    )
```

profile of v0, /device:TPU:0, one launch (start us, length us, event | category | flops | bytes accessed | tf_op | source)
XLA Modules:
  0.0 262.5 jit_solution(7148002226130458398)
XLA Ops:
  7.2 0.0 copy-start
  7.2 0.0 all-reduce.7.cloned.1.call-start
  7.2 2.5 fusion.22
  9.8 0.0 all-reduce.7.cloned.1.call-update
  9.8 0.0 all-reduce.9.cloned.1.call-start
  9.9 0.3 fusion.41
  10.2 0.3 fusion.39
  10.4 0.6 add_select_fusion
  11.0 34.6 %all-reduce.7.cloned.1.call-done = f32[64,768]{1,0:T(8,128)} async-done(((f32[64,768]{1,0:T(8,128)}), f32[64,768]{1,0:T(8,128)}) %all-reduce.7.cloned.1.call-update) | async-done | bytes 196624 | tf_op jit(solution)/shard_map/psum | solution.py:28
  45.7 2.1 fusion.11
  47.8 1.6 collective-permute-start
  49.4 1.0 fusion.40
  50.3 3.2 %collective-permute-done = f32[64,768]{1,0:T(8,128)S(1)} collective-permute-done((f32[64,768]{1,0:T(8,128)S(1)}, f32[64,768]{1,0:T(8,128)S(1)}, u32[]{:S(2)}, u32[]{:S(2)}) %collective-permute-start) | collective-permute-done | bytes 196640 | tf_op jit(solution)/shard_map/ppermute | solution.py:12
  53.6 0.0 copy-start.9
  53.6 2.5 collective-permute-start.1
  56.0 1.7 fusion.37
  57.7 5.2 %collective-permute-done.1 = f32[64,768]{1,0:T(8,128)S(1)} collective-permute-done((f32[64,768]{1,0:T(8,128)S(1)}, f32[64,768]{1,0:T(8,128)S(1)}, u32[]{:S(2)}, u32[]{:S(2)}) %collective-permute-start.1) | collective-permute-done | bytes 196640 | tf_op jit(solution)/shard_map/ppermute | solution.py:12
  62.9 2.3 fusion.19
  65.2 0.0 all-reduce.9.cloned.1.call-update
  65.2 0.0 all-reduce.11.cloned.1.call-start
  65.3 1.0 fusion.38
  66.3 32.6 %all-reduce.9.cloned.1.call-done = f32[64,768]{1,0:T(8,128)} async-done(((f32[64,768]{1,0:T(8,128)}), f32[64,768]{1,0:T(8,128)}) %all-reduce.9.cloned.1.call-update) | async-done | bytes 196624 | tf_op jit(solution)/shard_map/psum | solution.py:28
  98.8 2.8 %fusion.9 = f32[64,768]{1,0:T(8,128)} fusion(bf16[768,24]{1,0:T(8,128)(2,1)S(1)} %fusion.39, bf16[3,768,768]{2,1,0:T(8,128)(2,1)} %param.12, s32[768]{0:T(1024)S(1)} %copy-done.10, f32[64,768]{1,0:T(8,128)} %all-reduce.9.cloned.1.call-done), kind=kOutput, calls=%fused_computation.15 | convolution fusion | flops 104466432 | bytes 1612800 | tf_op jit(solution)/shard_map/dot_general | solution.py:58
  101.7 2.2 fusion.33
  103.9 1.6 collective-permute-start.2
  105.4 1.0 fusion.36
  106.4 3.2 %collective-permute-done.2 = f32[64,768]{1,0:T(8,128)S(1)} collective-permute-done((f32[64,768]{1,0:T(8,128)S(1)}, f32[64,768]{1,0:T(8,128)S(1)}, u32[]{:S(2)}, u32[]{:S(2)}) %collective-permute-start.2) | collective-permute-done | bytes 196640 | tf_op jit(solution)/shard_map/ppermute | solution.py:12
  109.6 1.0 add.63
  110.6 2.5 collective-permute-start.3
  113.0 2.8 %fusion.7 = f32[64,768]{1,0:T(8,128)} fusion(bf16[768,24]{1,0:T(8,128)(2,1)} %fusion.37, bf16[3,768,768]{2,1,0:T(8,128)(2,1)} %param.14, s32[768]{0:T(1024)} %add_select_fusion, f32[64,768]{1,0:T(8,128)S(1)} %copy-done.4), kind=kOutput, calls=%fused_computation.13 | convolution fusion | flops 104466432 | bytes 1773568 | tf_op jit(solution)/shard_map/dot_general | solution.py:69
  115.9 4.1 %collective-permute-done.3 = f32[64,768]{1,0:T(8,128)} collective-permute-done((f32[64,768]{1,0:T(8,128)S(1)}, f32[64,768]{1,0:T(8,128)}, u32[]{:S(2)}, u32[]{:S(2)}) %collective-permute-start.3) | collective-permute-done | bytes 196640 | tf_op jit(solution)/shard_map/ppermute | solution.py:12
  120.0 2.4 fusion.15
  122.4 0.0 all-reduce.11.cloned.1.call-update
  122.4 0.0 all-reduce.13.cloned.1.call-start
  122.5 2.1 fusion.34
  124.6 31.4 %all-reduce.11.cloned.1.call-done = f32[64,768]{1,0:T(8,128)} async-done(((f32[64,768]{1,0:T(8,128)}), f32[64,768]{1,0:T(8,128)}) %all-reduce.11.cloned.1.call-update) | async-done | bytes 196624 | tf_op jit(solution)/shard_map/psum | solution.py:28
  156.0 2.8 %fusion.35 = f32[64,768]{1,0:T(8,128)} fusion(f32[64,768]{1,0:T(8,128)S(1)} %fusion.34, bf16[768,24]{1,0:T(8,128)(2,1)S(1)} %copy-done.6, bf16[3,768,768]{2,1,0:T(8,128)(2,1)} %param.14, s32[768]{0:T(1024)S(1)} %copy-done.11, f32[64,768]{1,0:T(8,128)} %all-reduce.11.cloned.1.call-done), kind=kOutput, calls=%fused_computation.41 | convolution fusion | flops 104515584 | bytes 1809408 | tf_op jit(solution)/shard_map/dot_general | solution.py:69
  158.9 0.0 all-reduce.13.cloned.1.call-update
  158.9 0.0 all-reduce.15.cloned.1.call-start
  158.9 35.1 %all-reduce.13.cloned.1.call-done = f32[64,768]{1,0:T(8,128)} async-done(((f32[64,768]{1,0:T(8,128)}), f32[64,768]{1,0:T(8,128)}) %all-reduce.13.cloned.1.call-update) | async-done | bytes 196624 | tf_op jit(solution)/shard_map/psum | solution.py:72
  194.0 0.0 all-reduce.15.cloned.1.call-update
  194.1 0.0 all-reduce.17.cloned.1.call-start
  194.1 24.1 %all-reduce.15.cloned.1.call-done = f32[64,768]{1,0:T(8,128)} async-done(((f32[64,768]{1,0:T(8,128)}), f32[64,768]{1,0:T(8,128)}) %all-reduce.15.cloned.1.call-update) | async-done | bytes 196624 | tf_op jit(solution)/shard_map/psum | solution.py:73
  218.3 2.2 fusion.62
  220.5 0.0 all-reduce.17.cloned.1.call-update
  220.5 0.9 pad_maximum_fusion
  221.4 32.5 %all-reduce.17.cloned.1.call-done = f32[64,1536]{1,0:T(8,128)} async-done(((f32[64,1536]{1,0:T(8,128)}), f32[64,1536]{1,0:T(8,128)}) %all-reduce.17.cloned.1.call-update) | async-done | bytes 393232 | tf_op jit(solution)/shard_map/psum | solution.py:28
  253.9 1.8 copy.16
  (24 shorter events, 0.1 us)
Async XLA Ops:
  7.2 211.1 %copy-start = (bf16[768,1536]{1,0:T(8,128)(2,1)S(1)}, bf16[768,1536]{1,0:T(8,128)(2,1)}, u32[]{:S(2)}) copy-start(bf16[768,1536]{1,0:T(8,128)(2,1)} %param.11) | copy-start | bytes 7077892
  7.2 2.7 %copy-start.8 = (s32[3,6,24]{2,1,0:T(8,128)S(1)}, s32[3,6,24]{2,1,0:T(8,128)}, u32[]{:S(2)}) copy-start(s32[3,6,24]{2,1,0:T(8,128)} %param.13) | copy-start | bytes 5188
  7.2 38.5 %all-reduce.7.cloned.1.call-start = ((), (), s32[]{:S(2)}) async-start(), calls=%async_computation | async-start | bytes 393216 | tf_op jit(solution)/shard_map/psum | solution.py:28
  9.8 89.0 %all-reduce.9.cloned.1.call-start = ((), (), s32[]{:S(2)}) async-start(), calls=%async_computation.1 | async-start | bytes 393216 | tf_op jit(solution)/shard_map/psum | solution.py:28
  11.0 51.9 %copy-start.1 = (f32[1,3,64,768]{3,2,1,0:T(8,128)S(1)}, f32[1,3,64,768]{3,2,1,0:T(8,128)}, u32[]{:S(2)}) copy-start(f32[1,3,64,768]{3,2,1,0:T(8,128)} %param.8) | copy-start | bytes 1769476
  47.8 5.7 %collective-permute-start = (f32[64,768]{1,0:T(8,128)S(1)}, f32[64,768]{1,0:T(8,128)S(1)}, u32[]{:S(2)}, u32[]{:S(2)}) collective-permute-start(f32[64,768]{1,0:T(8,128)S(1)} %fusion.11), channel_id=1, source_target_pairs={{0,1},{1,0},{2,3},{3,2},{4,5},{5,4},{6,7},{7,6},{8,9},{9,8},{10,11... | collective-permute-start | bytes 589832 | tf_op jit(solution)/shard_map/ppermute | solution.py:12
  53.6 11.7 %copy-start.9 = (s32[3,6,24]{2,1,0:T(8,128)S(1)}, s32[3,6,24]{2,1,0:T(8,128)}, u32[]{:S(2)}) copy-start(s32[3,6,24]{2,1,0:T(8,128)} %param.15) | copy-start | bytes 5188
  53.6 9.4 %collective-permute-start.1 = (f32[64,768]{1,0:T(8,128)S(1)}, f32[64,768]{1,0:T(8,128)S(1)}, u32[]{:S(2)}, u32[]{:S(2)}) collective-permute-start(f32[64,768]{1,0:T(8,128)S(1)} %add.60), channel_id=1, source_target_pairs={{0,2},{1,3},{2,0},{3,1},{4,6},{5,7},{6,4},{7,5},{8,10},{9,11},{10,... | collective-permute-start | bytes 589832 | tf_op jit(solution)/shard_map/ppermute | solution.py:12
  57.7 41.1 %copy-start.10 = (s32[768]{0:T(1024)S(1)}, s32[768]{0:T(1024)}, u32[]{:S(2)}) copy-start(s32[768]{0:T(1024)} %add_select_fusion) | copy-start | bytes 9220
  65.2 36.4 %copy-start.3 = (f32[64,768]{1,0:T(8,128)S(1)}, f32[64,768]{1,0:T(8,128)}, u32[]{:S(2)}) copy-start(f32[64,768]{1,0:T(8,128)} %all-reduce.7.cloned.1.call-done) | copy-start | bytes 589828
  65.2 90.8 %all-reduce.11.cloned.1.call-start = ((), (), s32[]{:S(2)}) async-start(), calls=%async_computation.2 | async-start | bytes 393216 | tf_op jit(solution)/shard_map/psum | solution.py:28
  101.7 11.4 %copy-start.4 = (f32[64,768]{1,0:T(8,128)S(1)}, f32[64,768]{1,0:T(8,128)}, u32[]{:S(2)}) copy-start(f32[64,768]{1,0:T(8,128)} %all-reduce.9.cloned.1.call-done) | copy-start | bytes 589828
  103.9 2.5 copy-start.7
  103.9 5.7 %collective-permute-start.2 = (f32[64,768]{1,0:T(8,128)S(1)}, f32[64,768]{1,0:T(8,128)S(1)}, u32[]{:S(2)}, u32[]{:S(2)}) collective-permute-start(f32[64,768]{1,0:T(8,128)S(1)} %fusion.33), channel_id=1, source_target_pairs={{0,1},{1,0},{2,3},{3,2},{4,5},{5,4},{6,7},{7,6},{8,9},{9,8},{10,11... | collective-permute-start | bytes 589832 | tf_op jit(solution)/shard_map/ppermute | solution.py:12
  110.6 9.5 %collective-permute-start.3 = (f32[64,768]{1,0:T(8,128)S(1)}, f32[64,768]{1,0:T(8,128)}, u32[]{:S(2)}, u32[]{:S(2)}) collective-permute-start(f32[64,768]{1,0:T(8,128)S(1)} %add.63), channel_id=1, source_target_pairs={{0,2},{1,3},{2,0},{3,1},{4,6},{5,7},{6,4},{7,5},{8,10},{9,11},{10,... | collective-permute-start | bytes 589832 | tf_op jit(solution)/shard_map/ppermute | solution.py:12
  115.9 6.6 %copy-start.11 = (s32[768]{0:T(1024)S(1)}, s32[768]{0:T(1024)}, u32[]{:S(2)}) copy-start(s32[768]{0:T(1024)} %add_select_fusion) | copy-start | bytes 9220
  122.4 33.6 %copy-start.6 = (bf16[768,24]{1,0:T(8,128)(2,1)S(1)}, bf16[768,24]{1,0:T(8,128)(2,1)}, u32[]{:S(2)}) copy-start(bf16[768,24]{1,0:T(8,128)(2,1)} %fusion.36) | copy-start | bytes 110596
  122.4 71.6 %all-reduce.13.cloned.1.call-start = ((), (), s32[]{:S(2)}) async-start(), calls=%async_computation.3 | async-start | bytes 393216 | tf_op jit(solution)/shard_map/psum | solution.py:72
  124.6 93.6 %copy-start.2 = (f32[64,768]{1,0:T(8,128)S(1)}, f32[64,768]{1,0:T(8,128)}, u32[]{:S(2)}) copy-start(f32[64,768]{1,0:T(8,128)} %param.9) | copy-start | bytes 589828
  158.9 59.4 %all-reduce.15.cloned.1.call-start = ((), (), s32[]{:S(2)}) async-start(), calls=%async_computation.4 | async-start | bytes 393216 | tf_op jit(solution)/shard_map/psum | solution.py:73
  194.1 26.4 %copy-start.5 = (f32[64,768]{1,0:T(8,128)S(1)}, f32[64,768]{1,0:T(8,128)}, u32[]{:S(2)}) copy-start(f32[64,768]{1,0:T(8,128)} %all-reduce.11.cloned.1.call-done) | copy-start | bytes 589828
  194.1 59.8 %all-reduce.17.cloned.1.call-start = ((), (), s32[]{:S(2)}) async-start(), calls=%async_computation.5 | async-start | bytes 786432 | tf_op jit(solution)/shard_map/psum | solution.py:28
Sparse Core Ops, SparseCore 0:
  10.9 34.7 all-reduce.6
  65.3 33.4 all-reduce.8
  122.6 33.4 all-reduce.10
  159.0 34.9 all-reduce.12
  196.2 22.0 all-reduce.14
  221.1 32.7 all-reduce.16
where the time goes:
time: 263 us
  waiting for transfers between devices  206 us (78%)
  matrix products  29.5 us (11%)
  between operations  14.3 us (5%)
  starting transfers between devices  8.29 us (3%)
    psum x4, waiting for transfers between devices, solve_block(): return lax.psum(partial_sum, 'prow')  131 us
    psum x1, waiting for transfers between devices, shards(): across = lax.psum(root_local, 'pcol')  35.1 us
    psum x1, waiting for transfers between devices, shards(): root_update = lax.psum(across, 'grid')  24.1 us
    ppermute x4, waiting for transfers between devices, from_partner(): lax.ppermute(shard, axis, [(i, i ^ 1 << bit) for i in range(lax.axis_size...  15.8 us
    dot_general x6, matrix products, shards(): jnp.dot(kept[source], factor_tile, preferred_element_type=jnp.float32)  14.9 us
    dot_general x4, matrix products, solve_block(): jnp.dot(residual.astype(jnp.bfloat16), inverse, preferred_element_type=jn...  9.38 us
    ppermute x4, starting transfers between devices, from_partner(): lax.ppermute(shard, axis, [(i, i ^ 1 << bit) for i in range(lax.axis_size...  8.05 us
  transfers between devices with their start and end apart: 10, of which 10 were waited for; matrix products, arithmetic and copies ran while one was open for 4% of the time, Pallas kernels for 0%

commit v1 on v0

v1 whole, which is shorter than its diff:
```python
import functools

import jax
import jax.numpy as jnp
from jax import lax
from jax.experimental import pallas as pl
from jax.experimental.pallas import tpu as pltpu
from jax.sharding import PartitionSpec as P

MESH = pl.DeviceIdType.MESH


def flip(index, distance):
    bit = 1
    while bit <= distance:
        if distance & bit:
            index = index + bit * (1 - 2 * lax.rem(lax.div(index, bit), 2))
        bit *= 2
    return index


def pair_of(level, source):
    return level * (level - 1) // 2 + source


def kernel(
    cfg,
    sub_rhs, root_rhs, diag_inverse, root_inverse, inner_factor, inner_mask, root_factor, root_mask,
    sub_out, root_out,
    rhs_v, root_rhs_v, diag_v, rinv_v, inner_v, root_v,
    part_p, recv_a, sum_a, recv_b, solved,
    part_r, recv_ra, sum_ra, recv_rb, solved_r,
    part_c, recv_rs, recv_x, full, early,
    load_sem, out_sem, send_p, recv_p, send_c, recv_c,
):
    levels, parts, owners, others, trees, bits, tile = (
        cfg["levels"], cfg["parts"], cfg["owners"], cfg["others"], cfg["trees"], cfg["bits"], cfg["tile"]
    )
    prow = lax.axis_index("prow")
    pcol = lax.axis_index("pcol")
    grid = lax.axis_index("grid")
    member = lax.rem(pcol, owners)
    tree = lax.div(pcol, owners)
    other = grid * trees + tree
    core = lax.rem(prow, 2)

    def prow_partner(bit):
        return {"prow": flip(prow, 1 << bit)}

    def pcol_partner(distance):
        return {"pcol": flip(pcol, distance)}

    def other_partner(distance):
        there = flip(other, distance)
        return {"grid": lax.div(there, trees), "pcol": lax.rem(there, trees) * owners + member}

    loads = {}

    def load(name, source, target):
        copy = pltpu.make_async_copy(source, target, load_sem.at[len(loads)])
        copy.start()
        loads[name] = copy

    load("rhs", sub_rhs.at[tree], rhs_v)
    load(("diag", 0), diag_inverse.at[0], diag_v.at[0])
    for level in range(1, levels):
        for source in range(level):
            if source == level - 1:
                load(("root", level - 1), root_factor.at[level - 1], root_v.at[level - 1])
            pair = pair_of(level, source)
            load(("inner", pair), inner_factor.at[pair], inner_v.at[pair])
        load(("diag", level), diag_inverse.at[level], diag_v.at[level])
    load(("root", levels - 1), root_factor.at[levels - 1], root_v.at[levels - 1])
    load("root_rhs", root_rhs, root_rhs_v)
    load("rinv", root_inverse, rinv_v)

    barrier = pltpu.get_barrier_semaphore()
    partners = [prow_partner(bit) for bit in range(bits)]
    partners += [pcol_partner(distance) for distance in range(1, owners)]
    partners += [other_partner(distance) for distance in range(1, others)]
    for partner in partners:
        pl.semaphore_signal(barrier, inc=1, device_id=partner, device_id_type=MESH)

    waited = set()

    def arrived(name):
        if name not in waited:
            waited.add(name)
            loads[name].wait()

    sends = []

    def send(source, target, send_sem, recv_sem, partner):
        copy = pltpu.make_async_remote_copy(
            src_ref=source, dst_ref=target, send_sem=send_sem, recv_sem=recv_sem,
            device_id=partner, device_id_type=MESH,
        )
        copy.start()
        sends.append(copy)
        return copy

    first_column = prow * (inner_v.shape[2] // tile)

    def mask_weights(kind, which):
        arrived((kind, which))
        weights, mask = (inner_v, inner_mask) if kind == "inner" else (root_v, root_mask)

        def mask_row(row, carry):
            rows = pl.ds(pl.multiple_of(row * tile, tile), tile)
            for column in range(weights.shape[2] // tile):
                columns = pl.ds(column * tile, tile)
                keep = mask[which, row, first_column + column].astype(jnp.float32)
                scale = jnp.full((tile, tile), keep, jnp.float32).astype(jnp.bfloat16)
                weights[which, rows, columns] = weights[which, rows, columns] * scale
            return carry

        lax.fori_loop(0, weights.shape[1] // tile, mask_row, 0)

    rows_of = [pl.ds(h * (rhs_v.shape[1] // parts), rhs_v.shape[1] // parts) for h in range(parts)]
    waits = {}
    outs = []

    def buffers(level):
        if level < levels:
            return [ref.at[level] for ref in (part_p, recv_a, sum_a, recv_b, solved)]
        return [part_r, recv_ra, sum_ra, recv_rb, solved_r]

    def solve(level, h):
        part, got, _, _, _ = buffers(level)
        if level < levels:
            arrived("rhs")
            residual = rhs_v[level, rows_of[h]]
        else:
            arrived("root_rhs")
            residual = root_rhs_v[rows_of[h]]
        if level > 0:
            for copy in waits.pop(("gather", level, h)):
                copy.wait_recv()
            update = full[level - 1, h]
            residual = residual - update.reshape(residual.shape)
        if level < levels:
            arrived(("diag", level))
            inverse = diag_v[level]
        else:
            arrived("rinv")
            inverse = rinv_v[...]
        product = jnp.dot(residual.astype(jnp.bfloat16), inverse, preferred_element_type=jnp.float32)
        part[h] = product.reshape(part.shape[1:])
        if level == 0 and h == 0:
            pl.semaphore_wait(barrier, len(partners))
        waits["a", level, h] = send(
            part.at[h, 1 - core], got.at[h], send_p.at[level, h, 0], recv_p.at[level, h, 0], prow_partner(0)
        )

    def chip_sum(level, h):
        part, got, total, far, _ = buffers(level)
        waits.pop(("a", level, h)).wait_recv()
        total[h, 0] = part[h, core] + got[h]
        waits["b", level, h] = send(
            total.at[h, 0], far.at[h, 0], send_p.at[level, h, 1], recv_p.at[level, h, 1], prow_partner(1)
        )

    def far_sum(level, h, bit):
        _, _, total, far, done = buffers(level)
        waits.pop(("b", level, h)).wait_recv()
        value = total[h, bit - 1] + far[h, bit - 1]
        if bit + 1 < bits:
            total[h, bit] = value
            waits["b", level, h] = send(
                total.at[h, bit], far.at[h, bit],
                send_p.at[level, h, bit + 1], recv_p.at[level, h, bit + 1], prow_partner(bit + 1),
            )
        else:
            done[h, core] = value
            waits["c", level, h] = send(
                done.at[h, core], done.at[h, core],
                send_p.at[level, h, bits], recv_p.at[level, h, bits], prow_partner(0),
            )

    def solution_here(level, h):
        done = buffers(level)[4]
        if ("c", level, h) in waits:
            waits.pop(("c", level, h)).wait_recv()
            for half in range(2):
                rows = done.shape[2]
                span = pl.ds(h * 2 * rows + half * rows, rows)
                target = sub_out.at[level, span] if level < levels else root_out.at[span]
                copy = pltpu.make_async_copy(done.at[h, half], target, out_sem.at[level, h, half])
                copy.start()
                outs.append(copy)

    def kept(level, h):
        value = solved[level, h]
        return value.reshape((-1, value.shape[-1])).astype(jnp.bfloat16)

    def weights_of(level, source):
        if level < levels:
            return inner_v[pair_of(level, source)]
        return root_v[source]

    def scatter(level, h):
        source = level - 1
        solution_here(source, h)
        product = jnp.dot(kept(source, h), weights_of(level, source), preferred_element_type=jnp.float32)
        if source > 0:
            product = product + early[level - 2, h]
        part_c[source, h] = product.reshape(part_c.shape[2:])
        copies = []
        for distance in range(owners - 1, 0, -1):
            copies.append(send(
                part_c.at[source, h, flip(member, distance)], recv_rs.at[source, h, distance],
                send_c.at[source, h, 0, distance], recv_c.at[source, h, 0, distance], pcol_partner(distance),
            ))
        waits["scatter", level, h] = copies

    def look_ahead(source, h):
        for level in range(source + 2, levels + 1):
            product = jnp.dot(kept(source, h), weights_of(level, source), preferred_element_type=jnp.float32)
            if source > 0:
                product = product + early[level - 2, h]
            early[level - 2, h] = product

    def gather(level, h, total):
        full[level - 1, h, member] = total
        copies = []
        for distance in range(owners - 1, 0, -1):
            copies.append(send(
                full.at[level - 1, h, member], full.at[level - 1, h, member],
                send_c.at[level - 1, h, 1, distance], recv_c.at[level - 1, h, 1, distance],
                pcol_partner(distance),
            ))
        waits["gather", level, h] = copies

    def reduce(level, h):
        total = part_c[level - 1, h, member]
        for copy, distance in zip(waits.pop(("scatter", level, h)), range(owners - 1, 0, -1)):
            copy.wait_recv()
            total = total + recv_rs[level - 1, h, distance]
        if level < levels or others == 1:
            gather(level, h, total)
            return
        recv_x[h, other] = total
        waits["others", level, h] = [
            send(
                recv_x.at[h, other], recv_x.at[h, other],
                send_c.at[level - 1, h, 2, distance], recv_c.at[level - 1, h, 2, distance],
                other_partner(distance),
            )
            for distance in range(1, others)
        ]

    def across(level, h):
        if ("others", level, h) not in waits:
            return
        for copy in waits.pop(("others", level, h)):
            copy.wait_recv()
        total = recv_x[h, 0]
        for index in range(1, others):
            total = total + recv_x[h, index]
        gather(level, h, total)

    def each(step, *args):
        for h in range(parts):
            step(args[0], h, *args[1:])

    for level in range(levels + 1):
        each(solve, level)
        if level == 0:
            mask_weights("inner", 0)
        each(chip_sum, level)
        if level < levels - 1:
            mask_weights("inner", level + 1)
        elif level < levels:
            mask_weights("root", level)
        for bit in range(1, bits):
            each(far_sum, level, bit)
        if level < levels:
            each(scatter, level + 1)
            if level + 1 < levels:
                mask_weights("root", level)
                each(look_ahead, level)
            each(reduce, level + 1)
            each(across, level + 1)
        else:
            each(solution_here, level)
    for copy in sends:
        copy.wait_send()
    for copy in outs:
        copy.wait()


def shards(sizes, *arrays):
    sub_rhs, root_rhs, diag_inverse, root_inverse, inner_factor, inner_mask, root_factor, root_mask = arrays
    levels, nrhs, here = sub_rhs.shape[1:]
    assert levels == 3 and sizes["prow"] >= 4
    columns = diag_inverse.shape[2]
    root_columns = root_inverse.shape[1]
    ns = here * sizes["prow"]
    owners = ns // columns
    trees = sizes["pcol"] // owners
    others = trees * sizes["grid"]
    bits = sizes["prow"].bit_length() - 1
    parts = 2 if nrhs // 2 // owners >= 8 else 1
    rows = nrhs // parts
    chunk = rows // owners
    cfg = dict(
        levels=levels, parts=parts, owners=owners, others=others, trees=trees, bits=bits,
        tile=inner_factor.shape[1] // inner_mask.shape[1],
    )
    f32 = jnp.float32

    def prow_buffers(lead, width):
        return [
            pltpu.VMEM((*lead, parts, 2, rows // 2, width), f32),
            pltpu.VMEM((*lead, parts, rows // 2, width), f32),
            pltpu.VMEM((*lead, parts, bits - 1, rows // 2, width), f32),
            pltpu.VMEM((*lead, parts, bits - 1, rows // 2, width), f32),
            pltpu.VMEM((*lead, parts, 2, rows // 2, width), f32),
        ]

    most = max(owners, others)
    dma = pltpu.SemaphoreType.DMA
    scratch = [
        pltpu.VMEM(sub_rhs.shape[1:], f32),
        pltpu.VMEM(root_rhs.shape, f32),
        pltpu.VMEM(diag_inverse.shape, jnp.bfloat16),
        pltpu.VMEM(root_inverse.shape, jnp.bfloat16),
        pltpu.VMEM(inner_factor.shape, jnp.bfloat16),
        pltpu.VMEM(root_factor.shape, jnp.bfloat16),
        *prow_buffers((levels,), columns),
        *prow_buffers((), root_columns),
        pltpu.VMEM((levels, parts, owners, chunk, here), f32),
        pltpu.VMEM((levels, parts, owners, chunk, here), f32),
        pltpu.VMEM((parts, others, chunk, here), f32),
        pltpu.VMEM((levels, parts, owners, chunk, here), f32),
        pltpu.VMEM((levels - 1, parts, rows, here), f32),
        dma((3 * levels + 3,)),
        dma((levels + 1, parts, 2)),
        dma((levels + 1, parts, bits + 1)),
        dma((levels + 1, parts, bits + 1)),
        dma((levels, parts, 3, most)),
        dma((levels, parts, 3, most)),
    ]
    anywhere = pl.BlockSpec(memory_space=pl.ANY)
    scalars = pl.BlockSpec(memory_space=pltpu.SMEM)
    return pl.pallas_call(
        functools.partial(kernel, cfg),
        out_shape=(
            jax.ShapeDtypeStruct((levels, nrhs, columns), f32),
            jax.ShapeDtypeStruct((nrhs, root_columns), f32),
        ),
        in_specs=[anywhere] * 5 + [scalars, anywhere, scalars],
        out_specs=(anywhere, anywhere),
        scratch_shapes=scratch,
        compiler_params=pltpu.CompilerParams(collective_id=0, has_side_effects=True),
    )(*arrays)


def solution(mesh):
    return jax.shard_map(
        functools.partial(shards, dict(mesh.shape)),
        mesh=mesh,
        in_specs=(
            P("grid", None, None, "prow"),
            P(None, "prow"),
            P(None, "prow", ("grid", "pcol")),
            P("prow", "grid"),
            P(None, ("grid", "pcol"), "prow"),
            P(None, ("grid", "pcol"), None),
            P(None, ("grid", "pcol"), "prow"),
            P(None, ("grid", "pcol"), None),
        ),
        out_specs=(P(None, None, ("grid", "pcol")), P(None, "grid")),
        check_vma=False,
    )
```

time: 263 us -> 71.9 us (0.27)
  waiting for transfers between devices: 206 us -> 0 us
  Pallas kernels: 0 us -> 67.2 us
  matrix products: 29.5 us -> 0 us
  between operations: 14.3 us -> 0.64 us
  starting transfers between devices: 8.29 us -> 0 us
    psum x6 -> x0, waiting for transfers between devices: 190 us -> none  [the longest x4 131 us: solve_block(): return lax.psum(partial_sum, 'prow')]
    pallas_call x0 -> x1, Pallas kernels: none -> 67.2 us  [shards(): pl.pallas_call(functools.partial(kernel, cfg), out_shape=(jax.ShapeDtypeS...]
    dot_general x16 -> x0, matrix products: 29.5 us -> none  [the longest x6 14.9 us: shards(): jnp.dot(kept[source], factor_tile, preferred_element_type=jnp.float32)]
    ppermute x4 -> x0, waiting for transfers between devices: 15.8 us -> none  [from_partner(): lax.ppermute(shard, axis, [(i, i ^ 1 << bit) for i in range(lax.axis_size...]
    ppermute x4 -> x0, starting transfers between devices: 8.05 us -> none  [from_partner(): lax.ppermute(shard, axis, [(i, i ^ 1 << bit) for i in range(lax.axis_size...]
  transfers between devices with their start and end apart: 10 -> 0, of which waited for: 10 -> 0; matrix products, arithmetic and copies ran while one was open for 4% -> 0% of each run, Pallas kernels for 0% -> 0%
where the time goes in v1:
time: 71.9 us; the launch traced here: 71.5 us
  Pallas kernels  67.2 us (93%)
  local copies, waits for them, and re-layouts  3.69 us (5%)
    pallas_call x1, Pallas kernels, shards(): pl.pallas_call(functools.partial(kernel, cfg), out_shape=(jax.ShapeDtypeS...  67.2 us
    unnamed x2, local copies, waits for them, and re-layouts  3.69 us

profile of v1, /device:TPU:0, one launch (start us, length us, event | category | flops | bytes accessed | tf_op | source)
XLA Modules:
  0.0 71.5 jit_solution(17831193483767083790)
XLA Ops:
  0.6 67.2 %shard_map.95 = (f32[3,64,768]{2,1,0:T(8,128)}, f32[64,1536]{1,0:T(8,128)}) custom-call(f32[1,3,64,768]{3,2,1,0:T(8,128)} %sub_rhs.1, f32[64,768]{1,0:T(8,128)} %root_rhs.1, bf16[3,768,768]{2,1,0:T(8,128)(2,1)} %diag_inverse.1, bf16[768,1536]{1,0:T(8,128)(2,1)} %root_inverse.1, bf16[3,768,768]{2,1,0:T(8,128)(2,1)} %inner_factor.1, s32[3,6,24]{2,1,0:T(8,128)} %inner_mask.1, ...), custom_call_target="tpu_custom_call" | custom-call | tf_op jit(solution)/shard_map/pallas_call | solution.py:346
  67.8 1.9 %copy.12 = f32[3,64,768]{2,1,0:T(8,128)} copy(f32[3,64,768]{2,1,0:T(8,128)} %get-tuple-element.4) | data formatting | bytes 1179648
  69.7 1.8 %copy.13 = f32[64,1536]{1,0:T(8,128)} copy(f32[64,1536]{1,0:T(8,128)} %get-tuple-element.5) | data formatting | bytes 786432

commit v2 on v1

--- a/solution.py
+++ b/solution.py
@@ -26,15 +26,15 @@
 def kernel(
     cfg,
     sub_rhs, root_rhs, diag_inverse, root_inverse, inner_factor, inner_mask, root_factor, root_mask,
-    sub_out, root_out,
+    solved, solved_r,
     rhs_v, root_rhs_v, diag_v, rinv_v, inner_v, root_v,
-    part_p, recv_a, sum_a, recv_b, solved,
-    part_r, recv_ra, sum_ra, recv_rb, solved_r,
-    part_c, recv_rs, recv_x, full, early,
-    load_sem, out_sem, send_p, recv_p, send_c, recv_c,
+    part_p, recv_a, sum_a, recv_b,
+    part_r, recv_ra, sum_ra, recv_rb,
+    part_c, recv_rs, recv_x, full, part_d, recv_d, full_d, early,
+    load_sem, send_p, recv_p, send_c, recv_c,
 ):
-    levels, parts, owners, others, trees, bits, tile = (
-        cfg["levels"], cfg["parts"], cfg["owners"], cfg["others"], cfg["trees"], cfg["bits"], cfg["tile"]
+    levels, parts, owners, others, trees, chips, tile, direct = (
+        cfg["levels"], cfg["parts"], cfg["owners"], cfg["others"], cfg["trees"], cfg["chips"], cfg["tile"], cfg["direct"]
     )
     prow = lax.axis_index("prow")
     pcol = lax.axis_index("pcol")
@@ -44,15 +44,17 @@
     other = grid * trees + tree
     core = lax.rem(prow, 2)
 
-    def prow_partner(bit):
-        return {"prow": flip(prow, 1 << bit)}
+    def prow_partner(distance):
+        return {"prow": flip(prow, distance)}
 
     def pcol_partner(distance):
         return {"pcol": flip(pcol, distance)}
 
-    def other_partner(distance):
+    def other_partner(distance, within=0):
         there = flip(other, distance)
-        return {"grid": lax.div(there, trees), "pcol": lax.rem(there, trees) * owners + member}
+        return {"grid": lax.div(there, trees), "pcol": lax.rem(there, trees) * owners + flip(member, within)}
+
+    everyone = [(far, near) for far in range(others) for near in range(owners - 1, -1, -1) if far or near]
 
     loads = {}
 
@@ -61,9 +63,10 @@
         copy.start()
         loads[name] = copy
 
-    load("rhs", sub_rhs.at[tree], rhs_v)
+    load(("rhs", 0), sub_rhs.at[tree, 0], rhs_v.at[0])
     load(("diag", 0), diag_inverse.at[0], diag_v.at[0])
     for level in range(1, levels):
+        load(("rhs", level), sub_rhs.at[tree, level], rhs_v.at[level])
         for source in range(level):
             if source == level - 1:
                 load(("root", level - 1), root_factor.at[level - 1], root_v.at[level - 1])
@@ -75,9 +78,12 @@
     load("rinv", root_inverse, rinv_v)
 
     barrier = pltpu.get_barrier_semaphore()
-    partners = [prow_partner(bit) for bit in range(bits)]
-    partners += [pcol_partner(distance) for distance in range(1, owners)]
-    partners += [other_partner(distance) for distance in range(1, others)]
+    partners = [prow_partner(distance) for distance in range(1, 2 * chips)]
+    if direct:
+        partners += [other_partner(far, near) for far, near in everyone]
+    else:
+        partners += [pcol_partner(distance) for distance in range(1, owners)]
+        partners += [other_partner(distance) for distance in range(1, others)]
     for partner in partners:
         pl.semaphore_signal(barrier, inc=1, device_id=partner, device_id_type=MESH)
 
@@ -118,7 +124,6 @@
 
     rows_of = [pl.ds(h * (rhs_v.shape[1] // parts), rhs_v.shape[1] // parts) for h in range(parts)]
     waits = {}
-    outs = []
 
     def buffers(level):
         if level < levels:
@@ -128,7 +133,7 @@
     def solve(level, h):
         part, got, _, _, _ = buffers(level)
         if level < levels:
-            arrived("rhs")
+            arrived(("rhs", level))
             residual = rhs_v[level, rows_of[h]]
         else:
             arrived("root_rhs")
@@ -136,8 +141,11 @@
         if level > 0:
             for copy in waits.pop(("gather", level, h)):
                 copy.wait_recv()
-            update = full[level - 1, h]
-            residual = residual - update.reshape(residual.shape)
+            if level == levels and direct:
+                update = jnp.concatenate([full_d[h, far].reshape((residual.shape[0], -1)) for far in range(others)], axis=1)
+            else:
+                update = full[level - 1, h].reshape(residual.shape)
+            residual = residual - update
         if level < levels:
             arrived(("diag", level))
             inverse = diag_v[level]
@@ -149,45 +157,32 @@
         if level == 0 and h == 0:
             pl.semaphore_wait(barrier, len(partners))
         waits["a", level, h] = send(
-            part.at[h, 1 - core], got.at[h], send_p.at[level, h, 0], recv_p.at[level, h, 0], prow_partner(0)
+            part.at[h], got.at[h], send_p.at[level, h, 0], recv_p.at[level, h, 0], prow_partner(1)
         )
 
     def chip_sum(level, h):
         part, got, total, far, _ = buffers(level)
         waits.pop(("a", level, h)).wait_recv()
-        total[h, 0] = part[h, core] + got[h]
-        waits["b", level, h] = send(
-            total.at[h, 0], far.at[h, 0], send_p.at[level, h, 1], recv_p.at[level, h, 1], prow_partner(1)
-        )
-
-    def far_sum(level, h, bit):
+        total[h, core] = part[h, core] + got[h, core]
+        waits["b", level, h] = [
+            send(
+                total.at[h, core], far.at[h, distance - 2],
+                send_p.at[level, h, distance], recv_p.at[level, h, distance], prow_partner(distance),
+            )
+            for distance in range(2, 2 * chips)
+        ]
+        total[h, 1 - core] = part[h, 1 - core] + got[h, 1 - core]
+
+    def far_sum(level, h):
         _, _, total, far, done = buffers(level)
-        waits.pop(("b", level, h)).wait_recv()
-        value = total[h, bit - 1] + far[h, bit - 1]
-        if bit + 1 < bits:
-            total[h, bit] = value
-            waits["b", level, h] = send(
-                total.at[h, bit], far.at[h, bit],
-                send_p.at[level, h, bit + 1], recv_p.at[level, h, bit + 1], prow_partner(bit + 1),
-            )
-        else:
-            done[h, core] = value
-            waits["c", level, h] = send(
-                done.at[h, core], done.at[h, core],
-                send_p.at[level, h, bits], recv_p.at[level, h, bits], prow_partner(0),
-            )
-
-    def solution_here(level, h):
-        done = buffers(level)[4]
-        if ("c", level, h) in waits:
-            waits.pop(("c", level, h)).wait_recv()
-            for half in range(2):
-                rows = done.shape[2]
-                span = pl.ds(h * 2 * rows + half * rows, rows)
-                target = sub_out.at[level, span] if level < levels else root_out.at[span]
-                copy = pltpu.make_async_copy(done.at[h, half], target, out_sem.at[level, h, half])
-                copy.start()
-                outs.append(copy)
+        copies = waits.pop(("b", level, h))
+        for cross in range(2):
+            half = core if cross == 0 else 1 - core
+            value = total[h, half]
+            for slot in range(cross, len(copies), 2):
+                copies[slot].wait_recv()
+                value = value + far[h, slot]
+            done[h, half] = value
 
     def kept(level, h):
         value = solved[level, h]
@@ -200,10 +195,22 @@
 
     def scatter(level, h):
         source = level - 1
-        solution_here(source, h)
         product = jnp.dot(kept(source, h), weights_of(level, source), preferred_element_type=jnp.float32)
         if source > 0:
             product = product + early[level - 2, h]
+        if level == levels and direct:
+            width = part_d.shape[-1]
+            for far in range(others):
+                part_d[h, far] = product[:, far * width:(far + 1) * width].reshape(part_d.shape[2:])
+            waits["scatter", level, h] = [
+                send(
+                    part_d.at[h, flip(other, far), flip(member, near)], recv_d.at[h, far, near],
+                    send_c.at[source, h, 2 * far, near], recv_c.at[source, h, 2 * far, near],
+                    other_partner(far, near),
+                )
+                for far, near in everyone
+            ]
+            return
         part_c[source, h] = product.reshape(part_c.shape[2:])
         copies = []
         for distance in range(owners - 1, 0, -1):
@@ -232,6 +239,21 @@
         waits["gather", level, h] = copies
 
     def reduce(level, h):
+        if level == levels and direct:
+            total = part_d[h, other, member]
+            for copy, (far, near) in zip(waits.pop(("scatter", level, h)), everyone):
+                copy.wait_recv()
+                total = total + recv_d[h, far, near]
+            full_d[h, other, member] = total
+            waits["gather", level, h] = [
+                send(
+                    full_d.at[h, other, member], full_d.at[h, other, member],
+                    send_c.at[level - 1, h, 2 * far + 1, near], recv_c.at[level - 1, h, 2 * far + 1, near],
+                    other_partner(far, near),
+                )
+                for far, near in everyone
+            ]
+            return
         total = part_c[level - 1, h, member]
         for copy, distance in zip(waits.pop(("scatter", level, h)), range(owners - 1, 0, -1)):
             copy.wait_recv()
@@ -272,8 +294,7 @@
             mask_weights("inner", level + 1)
         elif level < levels:
             mask_weights("root", level)
-        for bit in range(1, bits):
-            each(far_sum, level, bit)
+        each(far_sum, level)
         if level < levels:
             each(scatter, level + 1)
             if level + 1 < levels:
@@ -281,12 +302,8 @@
                 each(look_ahead, level)
             each(reduce, level + 1)
             each(across, level + 1)
-        else:
-            each(solution_here, level)
     for copy in sends:
         copy.wait_send()
-    for copy in outs:
-        copy.wait()
 
 
 def shards(sizes, *arrays):
@@ -299,23 +316,25 @@
     owners = ns // columns
     trees = sizes["pcol"] // owners
     others = trees * sizes["grid"]
-    bits = sizes["prow"].bit_length() - 1
+    chips = sizes["prow"] // 2
     parts = 2 if nrhs // 2 // owners >= 8 else 1
     rows = nrhs // parts
     chunk = rows // owners
+    direct = others > 1 and here % (others * 128) == 0
+    width = here // others if direct else 128
     cfg = dict(
-        levels=levels, parts=parts, owners=owners, others=others, trees=trees, bits=bits,
-        tile=inner_factor.shape[1] // inner_mask.shape[1],
+        levels=levels, parts=parts, owners=owners, others=others, trees=trees, chips=chips,
+        tile=inner_factor.shape[1] // inner_mask.shape[1], direct=direct,
     )
     f32 = jnp.float32
 
     def prow_buffers(lead, width):
+        half = (rows // 2, width)
         return [
-            pltpu.VMEM((*lead, parts, 2, rows // 2, width), f32),
-            pltpu.VMEM((*lead, parts, rows // 2, width), f32),
-            pltpu.VMEM((*lead, parts, bits - 1, rows // 2, width), f32),
-            pltpu.VMEM((*lead, parts, bits - 1, rows // 2, width), f32),
-            pltpu.VMEM((*lead, parts, 2, rows // 2, width), f32),
+            pltpu.VMEM((*lead, parts, 2, *half), f32),
+            pltpu.VMEM((*lead, parts, 2, *half), f32),
+            pltpu.VMEM((*lead, parts, 2, *half), f32),
+            pltpu.VMEM((*lead, parts, 2 * chips - 2, *half), f32),
         ]
 
     most = max(owners, others)
@@ -333,27 +352,30 @@
         pltpu.VMEM((levels, parts, owners, chunk, here), f32),
         pltpu.VMEM((parts, others, chunk, here), f32),
         pltpu.VMEM((levels, parts, owners, chunk, here), f32),
+        pltpu.VMEM((parts, others, owners, chunk, width), f32),
+        pltpu.VMEM((parts, others, owners, chunk, width), f32),
+        pltpu.VMEM((parts, others, owners, chunk, width), f32),
         pltpu.VMEM((levels - 1, parts, rows, here), f32),
-        dma((3 * levels + 3,)),
-        dma((levels + 1, parts, 2)),
-        dma((levels + 1, parts, bits + 1)),
-        dma((levels + 1, parts, bits + 1)),
-        dma((levels, parts, 3, most)),
-        dma((levels, parts, 3, most)),
+        dma((levels * (levels - 1) // 2 + 3 * levels + 2,)),
+        dma((levels + 1, parts, 2 * chips)),
+        dma((levels + 1, parts, 2 * chips)),
+        dma((levels, parts, max(3, 2 * others), most)),
+        dma((levels, parts, max(3, 2 * others), most)),
     ]
     anywhere = pl.BlockSpec(memory_space=pl.ANY)
     scalars = pl.BlockSpec(memory_space=pltpu.SMEM)
-    return pl.pallas_call(
+    sub_out, root_out = pl.pallas_call(
         functools.partial(kernel, cfg),
         out_shape=(
-            jax.ShapeDtypeStruct((levels, nrhs, columns), f32),
-            jax.ShapeDtypeStruct((nrhs, root_columns), f32),
+            pltpu.VMEM((levels, parts, 2, rows // 2, columns), f32),
+            pltpu.VMEM((parts, 2, rows // 2, root_columns), f32),
         ),
         in_specs=[anywhere] * 5 + [scalars, anywhere, scalars],
-        out_specs=(anywhere, anywhere),
+        out_specs=(pl.BlockSpec(memory_space=pltpu.VMEM), pl.BlockSpec(memory_space=pltpu.VMEM)),
         scratch_shapes=scratch,
         compiler_params=pltpu.CompilerParams(collective_id=0, has_side_effects=True),
     )(*arrays)
+    return sub_out.reshape((levels, nrhs, columns)), root_out.reshape((nrhs, root_columns))
 
 
 def solution(mesh):

time: 71.9 us -> 77.6 us (1.079)
  Pallas kernels: 67.2 us -> 75.1 us
  local copies, waits for them, and re-layouts: 3.69 us -> 1.56 us
    pallas_call x1, Pallas kernels: 67.2 us -> 75.1 us  [shards(): pl.pallas_call(functools.partial(kernel, cfg), out_shape=(pltpu.VMEM((lev...]
    unnamed x2, local copies, waits for them, and re-layouts: 3.69 us -> 1.56 us
where the time goes in v2:
time: 77.6 us; the launch traced here: 77.3 us
  Pallas kernels  75.1 us (97%)
  local copies, waits for them, and re-layouts  1.56 us (2%)
    pallas_call x1, Pallas kernels, shards(): pl.pallas_call(functools.partial(kernel, cfg), out_shape=(pltpu.VMEM((lev...  75.1 us
    unnamed x2, local copies, waits for them, and re-layouts  1.56 us

profile of v2, /device:TPU:0, one launch (start us, length us, event | category | flops | bytes accessed | tf_op | source)
XLA Modules:
  0.0 77.3 jit_solution(7646930559387402159)
XLA Ops:
  0.6 75.1 %shard_map.95 = (f32[3,2,2,16,768]{4,3,2,1,0:T(8,128)S(1)}, f32[2,2,16,1536]{3,2,1,0:T(8,128)S(1)}) custom-call(f32[1,3,64,768]{3,2,1,0:T(8,128)} %sub_rhs.1, f32[64,768]{1,0:T(8,128)} %root_rhs.1, bf16[3,768,768]{2,1,0:T(8,128)(2,1)} %diag_inverse.1, bf16[768,1536]{1,0:T(8,128)(2,1)} %root_inverse.1, bf16[3,768,768]{2,1,0:T(8,128)(2,1)} %inner_factor.1, ...), custom_call_target="tpu_custom_call" | custom-call | tf_op jit(solution)/shard_map/pallas_call | solution.py:367
  75.7 0.8 %copy.12 = f32[3,64,768]{2,1,0:T(8,128)} copy(f32[3,64,768]{2,1,0:T(8,128)S(1)} %bitcast.2) | data formatting | bytes 1179648
  76.6 0.7 copy.13
